TPU v7x, 32 devices: a whole 2x2x4 slice. The times are simulated.
32 devices in a mesh: row: 4 (over z), col: 8 (over y, x, core).
Axes of the slice: x: 2, y: 2, z: 4, core: 2. Of those that a mesh axis runs over, the one named last changes fastest.
Arguments:
- a_matrix: bfloat16 [8192, 8192], P('row', 'col'), may hold values from -6 to 6
- a_flags: int32 [64, 64], P('row', 'col'), may hold values from 0 to 1, as said below
- b_matrix: bfloat16 [8192, 16384], P('row', 'col'), may hold values from -0.1875 to 0.1875
- b_flags: int32 [64, 128], P('row', 'col'), may hold values from 0 to 1, as said below
- sections: int32 [2], replicated, may hold values from 0 to 7
Outputs:
- packed: bfloat16 [8192, 16384], P('row', 'col')
- tile_place: int32 [64, 128], P('row', 'col')
Inputs may be any that keep to these rules, and one draw needn't show every extreme that they name: `a_flags`: 0 or 1; the 16 x 8 tiles of one device hold at most 64 ones, and some device holds exactly 64. `b_flags`: 0 or 1; each aligned block of 8 x 16 tiles holds at most 64 ones, and some block exactly 64.
All inputs are finite; a program needn't handle non-finite values.
Results may differ from a plain program's by a relative error of at most 0.001.
Values may be sent and summed in bfloat16 or wider, within the bound.
No kernel may reach another device: no remote copies, remote signals or barrier semaphores. Data moves between devices by JAX's collectives and lax.ppermute only.
A program may use at most 128 MiB of HBM per device.

v0:
```python
import jax
import jax.numpy as jnp
from jax import lax
from jax.sharding import PartitionSpec as P

TILE = 128
SECTIONS = 2
MOST = 64


def spread(value, axis, source):
    kept = jnp.where(lax.axis_index(axis) == source, value, 0).astype(value.dtype)
    return lax.psum(kept, axis)


def prefix(value, axis, combine, identity):
    length, position = (lax.axis_size(axis), lax.axis_index(axis))
    everything = lax.all_gather(value, axis)
    start = jnp.broadcast_to(jnp.asarray(identity, value.dtype), value.shape)

    def lap(k, before):
        reached = k < position
        new = combine(before, everything[k])
        return jnp.where(reached, new, before)

    return lax.fori_loop(0, length, lap, start)


def to_tiles(matrix, tile_rows, tile_cols):
    return (
        matrix.reshape(tile_rows, TILE, tile_cols, TILE)
        .transpose(0, 2, 1, 3)
        .reshape(tile_rows * tile_cols, TILE, TILE)
    )


def from_tiles(tiles, tile_rows, tile_cols):
    return (
        tiles.reshape(tile_rows, tile_cols, TILE, TILE)
        .transpose(0, 2, 1, 3)
        .reshape(tile_rows * TILE, tile_cols * TILE)
    )


def mask_tiles(matrix, flags, tile_rows, tile_cols):
    shaped = matrix.reshape(tile_rows, TILE, tile_cols, TILE)
    shaped = shaped * flags[:, None, :, None]
    return shaped.reshape(tile_rows * TILE, tile_cols * TILE)


def compact(tiles, flags_flat, capacity):
    rank_of = jnp.cumsum(flags_flat) - 1
    slot_ids = jnp.arange(capacity, dtype=jnp.int32)
    matched = (flags_flat[None, :] == 1) & (rank_of[None, :] == slot_ids[:, None])
    source = jnp.sum(
        jnp.where(matched, jnp.arange(flags_flat.shape[0], dtype=jnp.int32)[None, :], 0), axis=1
    )
    is_valid = jnp.any(matched, axis=1)
    return jnp.take(tiles, source, axis=0) * is_valid.astype(tiles.dtype)[:, None, None]


def expand(packed_tiles, flags_flat, capacity):
    rank_of = jnp.cumsum(flags_flat) - 1
    position = jnp.where(flags_flat == 1, rank_of, capacity)
    extended = jnp.concatenate(
        [packed_tiles, jnp.zeros((1, TILE, TILE), packed_tiles.dtype)], axis=0
    )
    return jnp.take(extended, position, axis=0)


def add_up(earlier, later):
    return earlier + later


def shards(a_matrix, a_flags, b_matrix, b_flags, sections):
    tile_rows, panel_cols = a_flags.shape
    tile_cols = b_flags.shape[1]
    row_ratio = lax.axis_size("col") // lax.axis_size("row")
    panel_width = panel_cols * TILE
    a_send_flags = a_flags.astype(jnp.bfloat16)
    product = jnp.zeros((tile_rows * TILE, tile_cols * TILE), jnp.float32)
    intersection = jnp.zeros((tile_rows, tile_cols), jnp.float32)
    for step_index in range(SECTIONS):
        section = sections[step_index]
        owner_row = section // row_ratio
        start_tile = section % row_ratio * panel_cols
        b_panel = lax.dynamic_slice_in_dim(b_matrix, start_tile * TILE, panel_width, 0)
        b_panel_flags = lax.dynamic_slice_in_dim(b_flags, start_tile, panel_cols, 0)
        b_send_flags = b_panel_flags.astype(jnp.bfloat16)
        a_packed = compact(to_tiles(a_matrix, tile_rows, panel_cols), a_flags.reshape(-1), MOST)
        b_packed = compact(
            to_tiles(b_panel, panel_cols, tile_cols), b_panel_flags.reshape(-1), MOST
        )
        a_recv, a_got_flags = (
            spread(a_packed, "col", section),
            spread(a_send_flags, "col", section),
        )
        b_recv, b_got_flags = (
            spread(b_packed, "row", owner_row),
            spread(b_send_flags, "row", owner_row),
        )
        a_got = from_tiles(
            expand(a_recv, a_got_flags.astype(jnp.int32).reshape(-1), MOST), tile_rows, panel_cols
        )
        b_got = from_tiles(
            expand(b_recv, b_got_flags.astype(jnp.int32).reshape(-1), MOST), panel_cols, tile_cols
        )
        a_masked = mask_tiles(a_got, a_got_flags, tile_rows, panel_cols)
        b_masked = mask_tiles(b_got, b_got_flags, panel_cols, tile_cols)
        product = product + jnp.dot(a_masked, b_masked, preferred_element_type=jnp.float32)
        intersection = intersection + jnp.dot(
            a_got_flags.astype(jnp.float32),
            b_got_flags.astype(jnp.float32),
            precision=lax.Precision.HIGHEST,
        )
    occupied = (intersection > 0.5).astype(jnp.int32).reshape(-1)
    filled = jnp.sum(occupied).reshape(1)
    zero_count = jnp.zeros((1,), jnp.int32)
    offset = prefix(filled, ("row", "col"), add_up, zero_count)
    tiles = to_tiles(product.astype(jnp.bfloat16), tile_rows, tile_cols)
    packed = from_tiles(compact(tiles, occupied, tile_rows * tile_cols), tile_rows, tile_cols)
    slot_ids = jnp.arange(tile_rows * tile_cols, dtype=jnp.int32)
    places = jnp.where(slot_ids < filled[0], offset[0] + slot_ids, -1).astype(jnp.int32)
    return (packed, places.reshape(tile_rows, tile_cols))


def solution(mesh):
    return jax.shard_map(
        shards,
        mesh=mesh,
        in_specs=(P("row", "col"), P("row", "col"), P("row", "col"), P("row", "col"), P()),
        out_specs=(P("row", "col"), P("row", "col")),
        check_vma=False,
    )
```

profile of v0, /device:TPU:0, one launch (start us, length us, event | category | flops | bytes accessed | tf_op | source)
XLA Modules:
  0.0 386.5 jit_solution(5069654762923967390)
XLA Ops:
  7.2 0.8 copy.70
  8.0 0.7 broadcast_compare_fusion.7
  9.5 1.3 fusion.23
  12.2 3.3 copy.90
  15.8 3.3 copy.72
  19.1 3.1 gather_fusion.1
  22.3 2.4 broadcast_select_fusion.4
  30.5 9.1 %dynamic-slice_bitcast_fusion = (bf16[128,8,16,128]{3,1,2,0:T(8,128)(2,1)S(1)}, bf16[128,8,16,128]{3,1,2,0:T(8,128)(2,1)}) fusion(bf16[2048,2048]{1,0:T(8,128)(2,1)} %param.13, s32[]{:T(128)S(6)} %select_n.201, s32[]{:T(128)S(6)} %select_n.193), kind=kLoop, calls=%fused_computation.29 | loop fusion | bytes 16777224
  39.6 1.4 copy.95
  41.0 0.7 bitcast_bitcast_fusion
  41.8 3.1 copy.86
  45.6 3.7 copy.92
  49.3 0.7 bitcast_bitcast_fusion.1
  50.0 3.2 copy.77
  53.7 3.1 gather_fusion.6
  56.9 4.7 %gather_fusion.3 = bf16[64,128,128]{2,1,0:T(8,128)(2,1)} fusion(bf16[128,128,128]{2,1,0:T(8,128)(2,1)} %bitcast.100, s32[1024]{0:T(1024)S(1)} %pad_clamp_fusion.5), kind=kCustom, calls=%fused_computation.2.clone | custom fusion | bytes 4194560 | tf_op jit(solution)/shard_map/jit(_take)/gather | solution.py:59
  61.6 1.7 fusion.10
  63.9 1.7 fusion.11
  65.6 13.2 %all-reduce.7 = (bf16[8,16]{1,0:T(8,128)(2,1)S(1)}, bf16[8,16]{1,0:T(8,128)(2,1)S(1)}) all-reduce(bf16[8,16]{1,0:T(8,128)(2,1)S(1)} %get-tuple-element.116, bf16[8,16]{1,0:T(8,128)(2,1)S(1)} %get-tuple-element.108), channel_id=1, replica_groups=mesh['row'=4,'col'=8] {'row'}, use_global_device_ids=true, to_apply=%region_1.2 | all-reduce | flops 256 | bytes 1024 | tf_op jit(solution)/shard_map/psum | solution.py:13
  78.8 11.8 %all-reduce.5 = (bf16[16,8]{0,1:T(8,128)(2,1)S(1)}, bf16[16,8]{0,1:T(8,128)(2,1)S(1)}) all-reduce(bf16[16,8]{0,1:T(8,128)(2,1)S(1)} %get-tuple-element.119, bf16[16,8]{0,1:T(8,128)(2,1)S(1)} %get-tuple-element.118), channel_id=1, replica_groups=mesh['row'=4,'col'=8] {'col'}, use_global_device_ids=true, to_apply=%region_0.1 | all-reduce | flops 256 | bytes 1024 | tf_op jit(solution)/shard_map/psum | solution.py:13
  91.3 0.7 reduce_sum.59
  94.3 0.7 dynamic-update-slice
  95.1 40.6 %all-reduce.4 = s32[32]{0:T(128)S(1)} all-reduce(s32[32]{0:T(128)S(1)} %dynamic-update-slice), channel_id=1, replica_groups=mesh['row'=4,'col'=8] {'row','col'}, use_global_device_ids=true, to_apply=%add.4 | all-reduce | flops 32 | bytes 256
  136.2 44.6 %while.13 = (s32[]{:T(128)}, s32[1]{0:T(128)}, s32[]{:T(128)}, s32[32,1]{0,1:T(1,128)S(1)}, s32[]{:T(128)}) while((s32[]{:T(128)}, s32[1]{0:T(128)}, s32[]{:T(128)}, s32[32,1]{0,1:T(1,128)S(1)}, s32[]{:T(128)}) %tuple.62), condition=%wide.region_27.30_spmd, body=%wide.region_26.29_spmd.sunk | while | flops 5 | bytes 107 | solution.py:26
  136.2 0.7 constant_dynamic-slice_fusion.6
  137.6 0.7 constant_dynamic-slice_fusion.6
  139.0 0.7 constant_dynamic-slice_fusion.6
  140.4 0.7 constant_dynamic-slice_fusion.6
  141.8 0.7 constant_dynamic-slice_fusion.6
  143.1 0.7 constant_dynamic-slice_fusion.6
  144.5 0.7 constant_dynamic-slice_fusion.6
  145.9 0.7 constant_dynamic-slice_fusion.6
  147.3 0.7 constant_dynamic-slice_fusion.6
  148.7 0.7 constant_dynamic-slice_fusion.6
  150.0 0.7 constant_dynamic-slice_fusion.6
  151.4 0.7 constant_dynamic-slice_fusion.6
  152.8 0.7 constant_dynamic-slice_fusion.6
  154.2 0.7 constant_dynamic-slice_fusion.6
  181.4 1.2 add_select_fusion
  182.6 1.9 concatenate.12
  184.9 1.5 concatenate.14
  186.4 3.1 gather_fusion.2
  189.5 4.6 %gather_fusion.5 = bf16[128,128,128]{2,1,0:T(8,128)(2,1)} fusion(bf16[65,128,128]{2,1,0:T(8,128)(2,1)} %concatenate.14, s32[1024]{0:T(1024)S(1)} %pad_clamp_fusion.3), kind=kCustom, calls=%fused_computation.5.clone | custom fusion | bytes 8389120 | tf_op jit(solution)/shard_map/jit(_take)/gather | solution.py:68
  194.1 3.2 broadcast_select_fusion.3
  197.3 1.0 copy-done
  198.8 4.4 %copy_multiply_fusion.3 = bf16[16,8,128,128]{3,1,2,0:T(8,128)(2,1)} fusion(bf16[16,8,128,128]{3,2,1,0:T(8,128)(2,1)S(1)} %bitcast.97, bf16[16,8]{1,0:T(8,128)(2,1)S(1)} %copy.73), kind=kLoop, calls=%fused_computation.28 | loop fusion | flops 2097152 | bytes 8388864 | tf_op jit(solution)/shard_map/mul | solution.py:47
  203.2 4.4 %copy_multiply_fusion.1 = bf16[16,8,128,128]{3,1,2,0:T(8,128)(2,1)} fusion(bf16[16,8,128,128]{3,2,1,0:T(8,128)(2,1)S(1)} %bitcast.98, bf16[16,8]{1,0:T(8,128)(2,1)S(1)} %copy.82), kind=kLoop, calls=%fused_computation.26 | loop fusion | flops 2097152 | bytes 8388864 | tf_op jit(solution)/shard_map/mul | solution.py:47
  207.5 59.3 %all-reduce.14.cloned.1.call-done = (bf16[64,128,128]{2,1,0:T(8,128)(2,1)}, bf16[64,128,128]{2,1,0:T(8,128)(2,1)}) async-done(((bf16[64,128,128]{2,1,0:T(8,128)(2,1)}, bf16[64,128,128]{2,1,0:T(8,128)(2,1)}), (bf16[64,128,128]{2,1,0:T(8,128)(2,1)}, bf16[64,128,128]{2,1,0:T(8,128)(2,1)})) %all-reduce.14.cloned.1.call-update) | async-done | bytes 4194320 | tf_op jit(solution)/shard_map/psum | solution.py:13
  266.9 1.8 concatenate.13
  268.6 3.1 gather_fusion.4
  271.7 2.6 broadcast_select_fusion.2
  274.4 4.3 %copy_multiply_fusion.2 = bf16[8,16,128,128]{3,1,2,0:T(8,128)(2,1)} fusion(bf16[8,16,128,128]{3,2,1,0:T(8,128)(2,1)S(1)} %bitcast.92, bf16[8,16]{1,0:T(8,128)(2,1)S(1)} %get-tuple-element.96), kind=kLoop, calls=%fused_computation.27 | loop fusion | flops 2097152 | bytes 8388864 | tf_op jit(solution)/shard_map/mul | solution.py:47
  278.9 3.2 gather_fusion.7
  282.1 2.6 broadcast_select_fusion
  284.8 2.3 copy_multiply_fusion
  287.1 1.1 copy-done.3
  288.2 11.7 %fusion.5 = f32[2048,2048]{1,0:T(8,128)} fusion(bf16[128,8,16,128]{3,2,1,0:T(8,128)(2,1)S(1)} %bitcast.103, bf16[256,8,8,128]{3,2,1,0:T(8,128)(2,1)S(1)} %bitcast.106), kind=kOutput, calls=%fused_computation.18 | convolution fusion | flops 8589934592 | bytes 25165824 | tf_op jit(solution)/shard_map/dot_general | solution.py:110
  299.9 16.3 %fusion = bf16[256,8,16,128]{3,1,2,0:T(8,128)(2,1)} fusion(f32[2048,2048]{1,0:T(8,128)} %fusion.5, bf16[128,8,16,128]{3,2,1,0:T(8,128)(2,1)S(1)} %bitcast.104, bf16[256,8,8,128]{3,2,1,0:T(8,128)(2,1)} %bitcast.107), kind=kOutput, calls=%fused_computation.10 | convolution fusion | flops 8598323200 | bytes 33554432 | tf_op jit(solution)/shard_map/dot_general | solution.py:110
  316.1 9.8 %copy.97 = bf16[256,8,16,128]{3,2,1,0:T(8,128)(2,1)} copy(bf16[256,8,16,128]{3,1,2,0:T(8,128)(2,1)} %fusion) | data formatting | bytes 16777216
  325.9 9.3 %copy.88 = bf16[16,128,16,128]{3,1,2,0:T(8,128)(2,1)} copy(bf16[16,128,16,128]{3,2,1,0:T(8,128)(2,1)} %bitcast.90) | data formatting | bytes 16777216 | tf_op jit(solution)/shard_map/reshape | solution.py:31
  335.2 12.0 %gather_fusion = bf16[256,128,128]{2,1,0:T(8,128)(2,1)} fusion(bf16[256,128,128]{2,1,0:T(8,128)(2,1)} %bitcast.89, s32[1024]{0:T(1024)S(1)} %pad_clamp_fusion), kind=kCustom, calls=%fused_computation.7 | custom fusion | bytes 16778240 | tf_op jit(solution)/shard_map/jit(_take)/gather | solution.py:59
  347.2 7.5 %multiply_bitcast_fusion = bf16[16,128,16,128]{3,1,2,0:T(8,128)(2,1)} fusion(bf16[16,16,128,128]{3,2,1,0:T(8,128)(2,1)} %bitcast.88, pred[16,16]{1,0:T(8,128)(4,1)S(1)} %compare_and_fusion, bf16[16,16]{1,0:T(8,128)(2,1)S(1)} %reshape.414), kind=kLoop, calls=%fused_computation.12 | loop fusion | flops 8388608 | bytes 16777984 | tf_op jit(solution)/shard_map/transpose | solution.py:40
  354.7 13.7 %copy.89 = bf16[16,128,16,128]{3,2,1,0:T(8,128)(2,1)} copy(bf16[16,128,16,128]{3,1,2,0:T(8,128)(2,1)} %multiply_bitcast_fusion) | data formatting | bytes 16777216 | tf_op jit(solution)/shard_map/transpose | solution.py:40
  368.4 11.1 %copy.120 = bf16[256,8,16,128]{3,1,2,0:T(8,128)(2,1)} copy(bf16[256,8,16,128]{3,2,1,0:T(8,128)(2,1)} %bitcast.91) | data formatting | bytes 16777216
  (127 shorter events, 20.5 us)
Async XLA Ops:
  7.2 175.5 %all-reduce.12.cloned.1.call-start = ((), (), s32[]{:S(2)}) async-start(), calls=%async_computation | async-start | bytes 8388608 | tf_op jit(solution)/shard_map/psum | solution.py:13
  22.3 8.0 %copy-start.7 = (s32[16,16]{1,0:T(8,128)S(1)}, s32[16,16]{1,0:T(8,128)}, u32[]{:S(2)}) copy-start(s32[16,16]{1,0:T(8,128)} %param.14) | copy-start | bytes 3076
  24.7 242.2 %all-reduce.14.cloned.1.call-start = ((), (), s32[]{:S(2)}) async-start(), calls=%async_computation.1 | async-start | bytes 8388608 | tf_op jit(solution)/shard_map/psum | solution.py:13
  61.6 2.3 copy-start.1
  63.9 14.9 %copy-start.6 = (s32[16,8]{0,1:T(8,128)S(1)}, s32[16,8]{0,1:T(8,128)}, u32[]{:S(2)}) copy-start(s32[16,8]{0,1:T(8,128)} %param.12) | copy-start | bytes 1540
  182.6 2.3 copy-start.4
  194.1 4.2 %copy-start = (bf16[128,128,128]{2,1,0:T(8,128)(2,1)S(1)}, bf16[128,128,128]{2,1,0:T(8,128)(2,1)}, u32[]{:S(2)}) copy-start(bf16[128,128,128]{2,1,0:T(8,128)(2,1)} %gather_fusion.5) | copy-start | bytes 12582916
  274.4 4.3 %copy-start.5 = (bf16[64,128,128]{2,1,0:T(8,128)(2,1)S(1)}, bf16[64,128,128]{2,1,0:T(8,128)(2,1)}, u32[]{:S(2)}) copy-start(bf16[64,128,128]{2,1,0:T(8,128)(2,1)} %get-tuple-element.99) | copy-start | bytes 6291460
  284.7 2.3 copy-start.2
  284.8 3.5 copy-start.3
Sparse Core Ops, SparseCore 0:
  24.8 84.2 all-reduce.11
  111.5 155.3 all-reduce.13
where the time goes:
time: 391 us; the launch traced here: 387 us
  local copies, waits for them, and re-layouts  145 us (37%)
  blocking collectives  65.6 us (17%)
  waiting for transfers between devices  59.4 us (15%)
  other arithmetic  43.6 us (11%)
  matrix products  28.3 us (7%)
  loops' own time  23.3 us (6%)
  between operations  21.6 us (6%)
    psum x2, waiting for transfers between devices, spread(): return lax.psum(kept, axis)  59.3 us
    unnamed x25, local copies, waits for them, and re-layouts  42.9 us
    unnamed x1, blocking collectives  40.6 us
    dot_general x2, matrix products, shards(): jnp.dot(a_masked, b_masked, preferred_element_type=jnp.float32)  27.9 us
    psum x2, blocking collectives, spread(): return lax.psum(kept, axis)  25 us
    another operation x1, loops' own time, prefix(): return lax.fori_loop(0, length, lap, start)  23.3 us
    gather x4, local copies, waits for them, and re-layouts, compact(): jnp.take(tiles, source, axis=0)  23 us
    dynamic_slice x32, local copies, waits for them, and re-layouts, lap(): new = combine(before, everything[k])  21.3 us
  transfers between devices with their start and end apart: 2, of which 1 were waited for; matrix products, arithmetic and copies ran while one was open for 22% of the time, Pallas kernels for 0%

commit v1 on v0

--- a/solution.py
+++ b/solution.py
@@ -10,7 +10,8 @@
 
 def spread(value, axis, source):
     kept = jnp.where(lax.axis_index(axis) == source, value, 0).astype(value.dtype)
-    return lax.psum(kept, axis)
+    _lay_frame = lambda view, peer_axis: jnp.sum(lax.all_gather(view, peer_axis), 0)
+    return _lay_frame(kept, axis)
 
 
 def prefix(value, axis, combine, identity):

time: 391 us -> 663 us (1.70)
  waiting for transfers between devices: 59.4 us -> 258 us
  blocking collectives: 65.6 us -> 97.7 us
  other arithmetic: 43.6 us -> 67.7 us
  local copies, waits for them, and re-layouts: 145 us -> 159 us
    all_gather x0 -> x4, waiting for transfers between devices: none -> 258 us  [spread(): lax.all_gather(view, peer_axis)]
    psum x2 -> x0, waiting for transfers between devices: 59.3 us -> none  [spread(): return lax.psum(kept, axis)]
    all_gather x0 -> x4, blocking collectives: none -> 49.6 us  [spread(): lax.all_gather(view, peer_axis)]
    reduce_sum x0 -> x8, other arithmetic: none -> 36.4 us  [spread(): jnp.sum(lax.all_gather(view, peer_axis), 0)]
    psum x2 -> x0, blocking collectives: 25 us -> none  [spread(): return lax.psum(kept, axis)]
    mul x0 -> x4, local copies, waits for them, and re-layouts: none -> 19.1 us  [mask_tiles(): shaped = shaped * flags[:, None, :, None]]
    mul x4, other arithmetic: 15.3 us -> 1.36 us  [mask_tiles(): shaped = shaped * flags[:, None, :, None]]
    unnamed x1, blocking collectives: 40.6 us -> 48.1 us
  transfers between devices with their start and end apart: 2 -> 4, of which waited for: 1 -> 3; matrix products, arithmetic and copies ran while one was open for 22% -> 16% of each run, Pallas kernels for 0% -> 0%
where the time goes in v1:
time: 663 us; the launch traced here: 654 us
  waiting for transfers between devices  258 us (39%)
  local copies, waits for them, and re-layouts  159 us (24%)
  blocking collectives  97.7 us (15%)
  other arithmetic  67.7 us (10%)
  matrix products  28.5 us (4%)
  between operations  21.4 us (3%)
  loops' own time  21.3 us (3%)
    all_gather x4, waiting for transfers between devices, spread(): lax.all_gather(view, peer_axis)  258 us
    all_gather x4, blocking collectives, spread(): lax.all_gather(view, peer_axis)  49.6 us
    unnamed x1, blocking collectives  48.1 us
    unnamed x17, local copies, waits for them, and re-layouts  38.7 us
    reduce_sum x8, other arithmetic, spread(): jnp.sum(lax.all_gather(view, peer_axis), 0)  36.4 us
    dot_general x2, matrix products, shards(): jnp.dot(a_masked, b_masked, preferred_element_type=jnp.float32)  28.1 us
    gather x4, local copies, waits for them, and re-layouts, compact(): jnp.take(tiles, source, axis=0)  21.8 us
    another operation x1, loops' own time, prefix(): return lax.fori_loop(0, length, lap, start)  21.3 us
  transfers between devices with their start and end apart: 4, of which 3 were waited for; matrix products, arithmetic and copies ran while one was open for 16% of the time, Pallas kernels for 0%

profile of v1, /device:TPU:0, one launch (start us, length us, event | category | flops | bytes accessed | tf_op | source)
XLA Modules:
  0.0 654.4 jit_solution(12607417675712547584)
XLA Ops:
  7.2 1.3 fusion.23
  13.9 0.7 convert_select_fusion
  16.0 8.3 %dynamic-slice_bitcast_fusion = (bf16[128,8,16,128]{3,1,2,0:T(8,128)(2,1)S(1)}, bf16[128,8,16,128]{3,1,2,0:T(8,128)(2,1)}) fusion(bf16[2048,2048]{1,0:T(8,128)(2,1)} %param.13, s32[]{:T(128)S(6)} %select_n.201, s32[]{:T(128)S(6)} %select_n.193), kind=kLoop, calls=%fused_computation.26 | loop fusion | bytes 16777224
  24.3 1.4 copy.115
  25.7 0.7 bitcast_bitcast_fusion
  26.4 3.1 copy.106
  29.5 3.1 gather_fusion.6
  32.6 1.6 fusion.10
  34.5 3.6 copy.112
  38.1 0.7 bitcast_bitcast_fusion.1
  38.8 3.2 copy.97
  42.0 3.4 gather_fusion.3
  45.4 1.7 fusion.11
  49.8 3.4 copy.110
  53.6 3.3 copy.92
  57.0 3.2 gather_fusion.1
  60.2 2.4 broadcast_select_fusion.4
  63.2 10.5 %all-gather.9 = bf16[8,16,8]{1,2,0:T(8,128)(2,1)S(1)} all-gather(bf16[1,16,8]{1,2,0:T(8,128)(2,1)S(1)} %get-tuple-element.110), channel_id=4, replica_groups=mesh['row'=4,'col'=8] {'col'}, dimensions={0}, use_global_device_ids=true | all-gather | bytes 2304 | tf_op jit(solution)/shard_map/all_gather | solution.py:13
  73.7 8.9 %all-gather.8 = bf16[8,16,8]{1,2,0:T(8,128)(2,1)S(1)} all-gather(bf16[1,16,8]{1,2,0:T(8,128)(2,1)S(1)} %get-tuple-element.111), channel_id=2, replica_groups=mesh['row'=4,'col'=8] {'col'}, dimensions={0}, use_global_device_ids=true | all-gather | bytes 2304 | tf_op jit(solution)/shard_map/all_gather | solution.py:13
  82.6 16.0 %all-gather.3 = bf16[32,16]{1,0:T(8,128)(2,1)S(1)} all-gather(bf16[8,16]{1,0:T(8,128)(2,1)S(1)} %get-tuple-element.96), channel_id=5, replica_groups=mesh['row'=4,'col'=8] {'row'}, dimensions={0}, use_global_device_ids=true | all-gather | bytes 1280 | tf_op jit(solution)/shard_map/all_gather | solution.py:13
  98.6 14.2 %all-gather.1 = bf16[32,16]{1,0:T(8,128)(2,1)S(1)} all-gather(bf16[8,16]{1,0:T(8,128)(2,1)S(1)} %get-tuple-element.108), channel_id=3, replica_groups=mesh['row'=4,'col'=8] {'row'}, dimensions={0}, use_global_device_ids=true | all-gather | bytes 1280 | tf_op jit(solution)/shard_map/all_gather | solution.py:13
  113.2 0.7 reduce_sum.163
  113.9 0.8 dynamic-update-slice
  114.7 48.1 %all-reduce.4 = s32[32]{0:T(128)S(1)} all-reduce(s32[32]{0:T(128)S(1)} %dynamic-update-slice), channel_id=1, replica_groups=mesh['row'=4,'col'=8] {'row','col'}, use_global_device_ids=true, to_apply=%add.4 | all-reduce | flops 32 | bytes 256
  166.0 41.7 %while.13 = (s32[]{:T(128)}, s32[1]{0:T(128)}, s32[]{:T(128)}, s32[32,1]{0,1:T(1,128)S(1)}, s32[]{:T(128)}) while((s32[]{:T(128)}, s32[1]{0:T(128)}, s32[]{:T(128)}, s32[32,1]{0,1:T(1,128)S(1)}, s32[]{:T(128)}) %tuple.64), condition=%wide.region_27.30_spmd, body=%wide.region_26.29_spmd.sunk | while | flops 5 | bytes 115 | solution.py:27
  167.4 0.6 constant_dynamic-slice_fusion.6
  169.9 0.6 constant_dynamic-slice_fusion.6
  173.8 0.6 constant_dynamic-slice_fusion.6
  176.4 0.6 constant_dynamic-slice_fusion.6
  179.0 0.6 constant_dynamic-slice_fusion.6
  182.9 0.6 constant_dynamic-slice_fusion.6
  185.5 0.6 constant_dynamic-slice_fusion.6
  208.3 1.3 add_select_fusion
  209.6 7.2 %reduce_sum.161 = bf16[64,128,128]{2,1,0:T(8,128)(2,1)} reduce(bf16[4,64,128,128]{3,2,1,0:T(8,128)(2,1)} %bitcast.120, bf16[]{:T(256)} %constant.142.clone.1), dimensions={0}, to_apply=%region_22.25 | reduce | flops 3145728 | bytes 10485762 | tf_op jit(solution)/shard_map/reduce_sum | solution.py:13
  216.8 1.8 concatenate.15
  218.6 3.1 gather_fusion.7
  221.7 2.6 broadcast_select_fusion
  224.6 4.8 copy.107
  229.4 108.0 %all-gather.17.cloned.1.call-done = bf16[256,128,128]{2,1,0:T(8,128)(2,1)} async-done(((bf16[64,128,128]{2,1,0:T(8,128)(2,1)}), bf16[256,128,128]{2,1,0:T(8,128)(2,1)}) %all-gather.17.cloned.1.call-update) | async-done | bytes 8388624 | tf_op jit(solution)/shard_map/all_gather | solution.py:13
  337.4 7.2 %reduce_sum.158 = bf16[64,128,128]{2,1,0:T(8,128)(2,1)} reduce(bf16[4,64,128,128]{3,2,1,0:T(8,128)(2,1)} %bitcast.121, bf16[]{:T(256)} %constant.142.clone.1), dimensions={0}, to_apply=%region_15.18 | reduce | flops 3145728 | bytes 10485762 | tf_op jit(solution)/shard_map/reduce_sum | solution.py:13
  344.6 2.2 concatenate.13
  346.8 3.1 gather_fusion.4
  349.9 2.6 broadcast_select_fusion.2
  352.9 5.3 copy.98
  358.1 69.1 %all-gather.19.cloned.1.call-done = bf16[512,128,128]{2,1,0:T(8,128)(2,1)} async-done(((bf16[64,128,128]{2,1,0:T(8,128)(2,1)}), bf16[512,128,128]{2,1,0:T(8,128)(2,1)}) %all-gather.19.cloned.1.call-update) | async-done | bytes 16777232 | tf_op jit(solution)/shard_map/all_gather | solution.py:13
  427.3 11.1 %reduce_sum.159 = bf16[64,128,128]{2,1,0:T(8,128)(2,1)} reduce(bf16[8,64,128,128]{3,2,1,0:T(8,128)(2,1)} %bitcast.110, bf16[]{:T(256)} %constant.142.clone.1), dimensions={0}, to_apply=%region_17.20 | reduce | flops 7340032 | bytes 18874370 | tf_op jit(solution)/shard_map/reduce_sum | solution.py:13
  438.4 80.4 %all-gather.15.cloned.1.call-done = bf16[512,128,128]{2,1,0:T(8,128)(2,1)} async-done(((bf16[64,128,128]{2,1,0:T(8,128)(2,1)}), bf16[512,128,128]{2,1,0:T(8,128)(2,1)}) %all-gather.15.cloned.1.call-update) | async-done | bytes 16777232 | tf_op jit(solution)/shard_map/all_gather | solution.py:13
  518.8 10.8 %reduce_sum.156 = bf16[64,128,128]{2,1,0:T(8,128)(2,1)} reduce(bf16[8,64,128,128]{3,2,1,0:T(8,128)(2,1)} %bitcast.111, bf16[]{:T(256)} %constant.142.clone.1), dimensions={0}, to_apply=%region_10.12 | reduce | flops 7340032 | bytes 18874370 | tf_op jit(solution)/shard_map/reduce_sum | solution.py:13
  529.6 1.9 concatenate.12
  531.8 1.5 concatenate.14
  533.3 4.6 gather_fusion.5
  537.9 2.6 broadcast_select_fusion.1
  540.9 5.5 copy.103
  546.4 3.0 gather_fusion.2
  549.4 2.6 broadcast_select_fusion.3
  552.4 3.6 copy.94
  556.0 11.9 %fusion.5 = f32[2048,2048]{1,0:T(8,128)} fusion(bf16[128,8,16,128]{3,2,1,0:T(8,128)(2,1)S(1)} %bitcast.125, bf16[256,8,8,128]{3,2,1,0:T(8,128)(2,1)S(1)} %bitcast.127), kind=kOutput, calls=%fused_computation.18 | convolution fusion | flops 8589934592 | bytes 25165824 | tf_op jit(solution)/shard_map/dot_general | solution.py:111
  567.9 16.3 %fusion = bf16[256,8,16,128]{3,1,2,0:T(8,128)(2,1)} fusion(f32[2048,2048]{1,0:T(8,128)} %fusion.5, bf16[128,8,16,128]{3,2,1,0:T(8,128)(2,1)S(1)} %bitcast.124, bf16[256,8,8,128]{3,2,1,0:T(8,128)(2,1)} %bitcast.126), kind=kOutput, calls=%fused_computation.10 | convolution fusion | flops 8598323200 | bytes 33554432 | tf_op jit(solution)/shard_map/dot_general | solution.py:111
  584.2 9.8 %copy.117 = bf16[256,8,16,128]{3,2,1,0:T(8,128)(2,1)} copy(bf16[256,8,16,128]{3,1,2,0:T(8,128)(2,1)} %fusion) | data formatting | bytes 16777216
  593.9 9.3 %copy.108 = bf16[16,128,16,128]{3,1,2,0:T(8,128)(2,1)} copy(bf16[16,128,16,128]{3,2,1,0:T(8,128)(2,1)} %bitcast.106) | data formatting | bytes 16777216 | tf_op jit(solution)/shard_map/reshape | solution.py:32
  603.2 12.0 %gather_fusion = bf16[256,128,128]{2,1,0:T(8,128)(2,1)} fusion(bf16[256,128,128]{2,1,0:T(8,128)(2,1)} %bitcast.105, s32[1024]{0:T(1024)S(1)} %pad_clamp_fusion), kind=kCustom, calls=%fused_computation.7 | custom fusion | bytes 16778240 | tf_op jit(solution)/shard_map/jit(_take)/gather | solution.py:60
  615.2 7.5 %multiply_bitcast_fusion = bf16[16,128,16,128]{3,1,2,0:T(8,128)(2,1)} fusion(bf16[16,16,128,128]{3,2,1,0:T(8,128)(2,1)} %bitcast.104, pred[16,16]{1,0:T(8,128)(4,1)S(1)} %compare_and_fusion, bf16[16,16]{1,0:T(8,128)(2,1)S(1)} %reshape.446), kind=kLoop, calls=%fused_computation.12 | loop fusion | flops 8388608 | bytes 16777984 | tf_op jit(solution)/shard_map/transpose | solution.py:41
  622.8 13.7 %copy.109 = bf16[16,128,16,128]{3,2,1,0:T(8,128)(2,1)} copy(bf16[16,128,16,128]{3,1,2,0:T(8,128)(2,1)} %multiply_bitcast_fusion) | data formatting | bytes 16777216 | tf_op jit(solution)/shard_map/transpose | solution.py:41
  636.4 11.1 %copy.136 = bf16[256,8,16,128]{3,1,2,0:T(8,128)(2,1)} copy(bf16[256,8,16,128]{3,2,1,0:T(8,128)(2,1)} %bitcast.107) | data formatting | bytes 16777216
  (139 shorter events, 25.6 us)
Async XLA Ops:
  7.2 202.4 %all-gather.21.cloned.1.call-start = ((), (), s32[]{:S(2)}) async-start(), calls=%async_computation.3 | async-start | bytes 10485760 | tf_op jit(solution)/shard_map/all_gather | solution.py:13
  34.3 303.1 %all-gather.17.cloned.1.call-start = ((), (), s32[]{:S(2)}) async-start(), calls=%async_computation.1 | async-start | bytes 10485760 | tf_op jit(solution)/shard_map/all_gather | solution.py:13
  45.4 3.6 copy-start.3
  47.2 380.1 %all-gather.19.cloned.1.call-start = ((), (), s32[]{:S(2)}) async-start(), calls=%async_computation.2 | async-start | bytes 18874368 | tf_op jit(solution)/shard_map/all_gather | solution.py:13
  62.6 456.1 %all-gather.15.cloned.1.call-start = ((), (), s32[]{:S(2)}) async-start(), calls=%async_computation | async-start | bytes 18874368 | tf_op jit(solution)/shard_map/all_gather | solution.py:13
  529.6 2.2 copy-start
  552.4 3.6 copy-start.2
  556.0 11.9 %copy-start.1 = (bf16[8,128,16,128]{3,2,1,0:T(8,128)(2,1)S(1)}, bf16[8,128,16,128]{3,2,1,0:T(8,128)(2,1)}, u32[]{:S(2)}) copy-start(bf16[8,128,16,128]{3,2,1,0:T(8,128)(2,1)} %copy.107) | copy-start | bytes 12582916
Sparse Core Ops, SparseCore 0:
  34.4 153.6 all-gather.20
  189.7 147.6 all-gather.16
  339.3 87.9 all-gather.18
  429.0 89.7 all-gather.14
